TPU v7x, 32 devices: a whole 2x2x4 slice. The times are simulated.
32 devices in a mesh: inp: 4 (over x, core), out: 8 (over z, y).
Axes of the slice: x: 2, y: 2, z: 4, core: 2. Of those that a mesh axis runs over, the one named last changes fastest.
Arguments:
- attention: bfloat16 [128, 16384], P(None, ('inp', 'out')), may hold values from -6 to 6
- residual: bfloat16 [128, 16384], P(None, 'out'), may hold values from -60 to 60
- wo_codes: int32 [2, 2048, 16384], P(None, 'inp', 'out'), may hold values from 0 to 255
- wo_books: bfloat16 [2, 256, 8], replicated, may hold values from -0.03125 to 0.03125
- wo_scale: float32 [16384], P('out'), may hold values from 0.5 to 2
- norm_gain: float32 [16384], replicated, may hold values from 0.25 to 1.75
- gate_codes: int32 [2, 2048, 53248], P(None, 'inp', 'out'), may hold values from 0 to 255
- gate_books: bfloat16 [2, 256, 8], replicated, may hold values from -0.03125 to 0.03125
- gate_scale: float32 [53248], P('out'), may hold values from 0.5 to 2
Outputs:
- stream: bfloat16 [128, 16384], P(None, 'out')
- gate_out: bfloat16 [128, 53248], P('inp', 'out')
All inputs are finite; a program needn't handle non-finite values.
Results may differ from a plain program's by a relative error of at most 0.0059.
Values may be sent and summed in bfloat16 or wider, within the bound.
No kernel may reach another device: no remote copies, remote signals or barrier semaphores. Data moves between devices by JAX's collectives and lax.ppermute only.
A program may use at most 192 MiB of HBM per device.

v0:
```python
import math

import jax
import jax.numpy as jnp
from jax import lax
from jax.sharding import PartitionSpec as P

D = 16384
BOOK = 256
GROUP = 8


epsilon = 1e-05


def unpack(codes, books, scale):
    groups, outputs = (codes.shape[1], codes.shape[2])
    block_size = math.gcd(groups, 16)
    block_count = groups // block_size
    tables = jnp.swapaxes(books, 1, 2)
    entries = lax.iota(jnp.int32, BOOK)

    def one_block(code_block):
        summed = jnp.zeros((block_size, GROUP, outputs), jnp.float32)
        for book in range(2):
            one_hot = (code_block[book][:, None, :] == entries[None, :, None]).astype(jnp.bfloat16)
            summed = summed + jnp.einsum(
                "ke,geo->gko", tables[book], one_hot, preferred_element_type=jnp.float32
            )
        weight = summed.reshape(block_size * GROUP, outputs) * scale[None, :]
        return weight.astype(jnp.bfloat16)

    code_blocks = jnp.swapaxes(codes.reshape(2, block_count, block_size, outputs), 0, 1)
    decoded = lax.map(one_block, code_blocks)
    return decoded.reshape(groups * GROUP, outputs)


def per_device(
    attention, residual, wo_codes, wo_books, wo_scale, norm_gain, gate_codes, gate_books, gate_scale
):
    features = lax.all_gather(attention, "out", axis=1, tiled=True)
    out_weight = unpack(wo_codes, wo_books, wo_scale)
    gate_weight = unpack(gate_codes, gate_books, gate_scale)
    summed = lax.psum(jnp.dot(features, out_weight, preferred_element_type=jnp.float32), "inp")
    hidden = residual.astype(jnp.float32) + summed
    block_width = hidden.shape[1]
    square_mean = lax.psum(jnp.sum(hidden * hidden, axis=1, keepdims=True), "out") / D
    gain_slice = lax.dynamic_slice_in_dim(
        norm_gain, lax.axis_index("out") * block_width, block_width, 0
    )
    normed_block = (hidden * lax.rsqrt(square_mean + epsilon) * gain_slice[None, :]).astype(
        jnp.bfloat16
    )
    everything = lax.all_gather(normed_block, "out", axis=1, tiled=True)
    input_width = features.shape[1]
    normed = lax.dynamic_slice_in_dim(
        everything, lax.axis_index("inp") * input_width, input_width, 1
    )
    stream = hidden.astype(jnp.bfloat16)
    gate_out = lax.psum_scatter(
        jnp.dot(normed, gate_weight, preferred_element_type=jnp.float32),
        "inp",
        scatter_dimension=0,
        tiled=True,
    ).astype(jnp.bfloat16)
    return (stream, gate_out)


def solution(mesh):
    placed = (
        P(None, ("inp", "out")),
        P(None, "out"),
        P(None, "inp", "out"),
        P(),
        P("out"),
        P(),
        P(None, "inp", "out"),
        P(),
        P("out"),
    )
    return jax.shard_map(
        per_device,
        mesh=mesh,
        in_specs=placed,
        out_specs=(P(None, "out"), P("inp", "out")),
        check_vma=False,
    )
```

profile of v0, /device:TPU:0, one launch (start us, length us, event | category | flops | bytes accessed | tf_op | source)
XLA Modules:
  0.0 1791.0 jit_solution(2096228655549355693)
XLA Ops:
  8.0 442.6 %while.24 = (s32[]{:T(128)}, bf16[32,128,2048]{2,1,0:T(8,128)(2,1)}, s32[32,2,16,2048]{3,2,0,1:T(8,128)}, bf16[2,8,256]{2,1,0:T(8,128)(2,1)}, f32[2048]{0:T(1024)}, /*index=5*/s32[]{:T(128)}) while((s32[]{:T(128)}, bf16[32,128,2048]{2,1,0:T(8,128)(2,1)}, s32[32,2,16,2048]{3,2,0,1:T(8,128)}, ...), condition=%wide.region_1.2_spmd.clone.clone, body=%wide.region_0.1_spmd.clone.clone.sunk | while | flops 285999104 | bytes 3948629 | solution.py:34
  463.3 38.1 %all-reduce.2.cloned.1.call-done = f32[128,2048]{0,1:T(8,128)} async-done(((f32[128,2048]{0,1:T(8,128)}), f32[128,2048]{0,1:T(8,128)}) %all-reduce.2.cloned.1.call-update) | async-done | bytes 1048592 | tf_op jit(solution)/shard_map/psum | solution.py:44
  503.0 21.4 %psum.15 = f32[128,1]{0,1:T(1,128)S(1)} all-reduce(f32[128,1]{0,1:T(1,128)S(1)} %bitcast.89), channel_id=1, replica_groups=mesh['inp'=4,'out'=8] {'out'}, use_global_device_ids=true, to_apply=%region_4.5 | all-reduce | flops 128 | bytes 1024 | tf_op jit(solution)/shard_map/psum | solution.py:47
  526.8 1197.7 %while.25 = (s32[]{:T(128)}, bf16[32,128,6656]{2,1,0:T(8,128)(2,1)}, s32[32,2,16,6656]{3,2,0,1:T(8,128)}, bf16[2,8,256]{2,1,0:T(8,128)(2,1)S(1)}, f32[6656]{0:T(1024)S(1)}, /*index=5*/s32[]{:T(128)}) while((s32[]{:T(128)}, bf16[32,128,6656]{2,1,0:T(8,128)(2,1)}, s32[32,2,16,6656]{3,2,0,1:T(8,128)}, ...), condition=%wide.region_6.7_spmd.clone.clone, body=%wide.region_5.6_spmd.clone.clone.sunk | while | flops 929497088 | bytes 12816469 | solution.py:34
  544.4 19.9 %fusion.52 = bf16[32,128,6656]{2,1,0:T(8,128)(2,1)} fusion(bf16[32,128,6656]{2,1,0:T(8,128)(2,1)} %get-tuple-element.265, s32[]{:T(128)S(6)} %copy.30, f32[16,6656,8]{1,2,0:T(8,128)S(1)} %fusion.51, s32[16,6656]{1,0:T(8,128)S(1)} %get-tuple-element.239, f32[6656]{0:T(1024)S(1)} %get-tuple-element.274, bf16[2,8,256]{2,1,0:T(8,128)(2,1)S(1)} %get-tuple-element.273), kind=kOutput, calls=%fused_computation.30.clone.1 | convolution fusion | flops 466026496 | bytes 5570564 | tf_op jit(solution)/shard_map/while/body/eval_jaxpr/ke,geo->gko/dot_general | solution.py:27
  581.8 19.9 %fusion.52 = bf16[32,128,6656]{2,1,0:T(8,128)(2,1)} fusion(bf16[32,128,6656]{2,1,0:T(8,128)(2,1)} %get-tuple-element.265, s32[]{:T(128)S(6)} %copy.30, f32[16,6656,8]{1,2,0:T(8,128)S(1)} %fusion.51, s32[16,6656]{1,0:T(8,128)S(1)} %get-tuple-element.239, f32[6656]{0:T(1024)S(1)} %get-tuple-element.274, bf16[2,8,256]{2,1,0:T(8,128)(2,1)S(1)} %get-tuple-element.273), kind=kOutput, calls=%fused_computation.30.clone.1 | convolution fusion | flops 466026496 | bytes 5570564 | tf_op jit(solution)/shard_map/while/body/eval_jaxpr/ke,geo->gko/dot_general | solution.py:27
  619.2 19.9 %fusion.52 = bf16[32,128,6656]{2,1,0:T(8,128)(2,1)} fusion(bf16[32,128,6656]{2,1,0:T(8,128)(2,1)} %get-tuple-element.265, s32[]{:T(128)S(6)} %copy.30, f32[16,6656,8]{1,2,0:T(8,128)S(1)} %fusion.51, s32[16,6656]{1,0:T(8,128)S(1)} %get-tuple-element.239, f32[6656]{0:T(1024)S(1)} %get-tuple-element.274, bf16[2,8,256]{2,1,0:T(8,128)(2,1)S(1)} %get-tuple-element.273), kind=kOutput, calls=%fused_computation.30.clone.1 | convolution fusion | flops 466026496 | bytes 5570564 | tf_op jit(solution)/shard_map/while/body/eval_jaxpr/ke,geo->gko/dot_general | solution.py:27
  694.0 19.9 %fusion.52 = bf16[32,128,6656]{2,1,0:T(8,128)(2,1)} fusion(bf16[32,128,6656]{2,1,0:T(8,128)(2,1)} %get-tuple-element.265, s32[]{:T(128)S(6)} %copy.30, f32[16,6656,8]{1,2,0:T(8,128)S(1)} %fusion.51, s32[16,6656]{1,0:T(8,128)S(1)} %get-tuple-element.239, f32[6656]{0:T(1024)S(1)} %get-tuple-element.274, bf16[2,8,256]{2,1,0:T(8,128)(2,1)S(1)} %get-tuple-element.273), kind=kOutput, calls=%fused_computation.30.clone.1 | convolution fusion | flops 466026496 | bytes 5570564 | tf_op jit(solution)/shard_map/while/body/eval_jaxpr/ke,geo->gko/dot_general | solution.py:27
  731.5 19.9 %fusion.52 = bf16[32,128,6656]{2,1,0:T(8,128)(2,1)} fusion(bf16[32,128,6656]{2,1,0:T(8,128)(2,1)} %get-tuple-element.265, s32[]{:T(128)S(6)} %copy.30, f32[16,6656,8]{1,2,0:T(8,128)S(1)} %fusion.51, s32[16,6656]{1,0:T(8,128)S(1)} %get-tuple-element.239, f32[6656]{0:T(1024)S(1)} %get-tuple-element.274, bf16[2,8,256]{2,1,0:T(8,128)(2,1)S(1)} %get-tuple-element.273), kind=kOutput, calls=%fused_computation.30.clone.1 | convolution fusion | flops 466026496 | bytes 5570564 | tf_op jit(solution)/shard_map/while/body/eval_jaxpr/ke,geo->gko/dot_general | solution.py:27
  768.9 19.9 %fusion.52 = bf16[32,128,6656]{2,1,0:T(8,128)(2,1)} fusion(bf16[32,128,6656]{2,1,0:T(8,128)(2,1)} %get-tuple-element.265, s32[]{:T(128)S(6)} %copy.30, f32[16,6656,8]{1,2,0:T(8,128)S(1)} %fusion.51, s32[16,6656]{1,0:T(8,128)S(1)} %get-tuple-element.239, f32[6656]{0:T(1024)S(1)} %get-tuple-element.274, bf16[2,8,256]{2,1,0:T(8,128)(2,1)S(1)} %get-tuple-element.273), kind=kOutput, calls=%fused_computation.30.clone.1 | convolution fusion | flops 466026496 | bytes 5570564 | tf_op jit(solution)/shard_map/while/body/eval_jaxpr/ke,geo->gko/dot_general | solution.py:27
  806.3 19.9 %fusion.52 = bf16[32,128,6656]{2,1,0:T(8,128)(2,1)} fusion(bf16[32,128,6656]{2,1,0:T(8,128)(2,1)} %get-tuple-element.265, s32[]{:T(128)S(6)} %copy.30, f32[16,6656,8]{1,2,0:T(8,128)S(1)} %fusion.51, s32[16,6656]{1,0:T(8,128)S(1)} %get-tuple-element.239, f32[6656]{0:T(1024)S(1)} %get-tuple-element.274, bf16[2,8,256]{2,1,0:T(8,128)(2,1)S(1)} %get-tuple-element.273), kind=kOutput, calls=%fused_computation.30.clone.1 | convolution fusion | flops 466026496 | bytes 5570564 | tf_op jit(solution)/shard_map/while/body/eval_jaxpr/ke,geo->gko/dot_general | solution.py:27
  843.7 19.9 %fusion.52 = bf16[32,128,6656]{2,1,0:T(8,128)(2,1)} fusion(bf16[32,128,6656]{2,1,0:T(8,128)(2,1)} %get-tuple-element.265, s32[]{:T(128)S(6)} %copy.30, f32[16,6656,8]{1,2,0:T(8,128)S(1)} %fusion.51, s32[16,6656]{1,0:T(8,128)S(1)} %get-tuple-element.239, f32[6656]{0:T(1024)S(1)} %get-tuple-element.274, bf16[2,8,256]{2,1,0:T(8,128)(2,1)S(1)} %get-tuple-element.273), kind=kOutput, calls=%fused_computation.30.clone.1 | convolution fusion | flops 466026496 | bytes 5570564 | tf_op jit(solution)/shard_map/while/body/eval_jaxpr/ke,geo->gko/dot_general | solution.py:27
  918.6 19.9 %fusion.52 = bf16[32,128,6656]{2,1,0:T(8,128)(2,1)} fusion(bf16[32,128,6656]{2,1,0:T(8,128)(2,1)} %get-tuple-element.265, s32[]{:T(128)S(6)} %copy.30, f32[16,6656,8]{1,2,0:T(8,128)S(1)} %fusion.51, s32[16,6656]{1,0:T(8,128)S(1)} %get-tuple-element.239, f32[6656]{0:T(1024)S(1)} %get-tuple-element.274, bf16[2,8,256]{2,1,0:T(8,128)(2,1)S(1)} %get-tuple-element.273), kind=kOutput, calls=%fused_computation.30.clone.1 | convolution fusion | flops 466026496 | bytes 5570564 | tf_op jit(solution)/shard_map/while/body/eval_jaxpr/ke,geo->gko/dot_general | solution.py:27
  956.0 19.9 %fusion.52 = bf16[32,128,6656]{2,1,0:T(8,128)(2,1)} fusion(bf16[32,128,6656]{2,1,0:T(8,128)(2,1)} %get-tuple-element.265, s32[]{:T(128)S(6)} %copy.30, f32[16,6656,8]{1,2,0:T(8,128)S(1)} %fusion.51, s32[16,6656]{1,0:T(8,128)S(1)} %get-tuple-element.239, f32[6656]{0:T(1024)S(1)} %get-tuple-element.274, bf16[2,8,256]{2,1,0:T(8,128)(2,1)S(1)} %get-tuple-element.273), kind=kOutput, calls=%fused_computation.30.clone.1 | convolution fusion | flops 466026496 | bytes 5570564 | tf_op jit(solution)/shard_map/while/body/eval_jaxpr/ke,geo->gko/dot_general | solution.py:27
  993.4 19.9 %fusion.52 = bf16[32,128,6656]{2,1,0:T(8,128)(2,1)} fusion(bf16[32,128,6656]{2,1,0:T(8,128)(2,1)} %get-tuple-element.265, s32[]{:T(128)S(6)} %copy.30, f32[16,6656,8]{1,2,0:T(8,128)S(1)} %fusion.51, s32[16,6656]{1,0:T(8,128)S(1)} %get-tuple-element.239, f32[6656]{0:T(1024)S(1)} %get-tuple-element.274, bf16[2,8,256]{2,1,0:T(8,128)(2,1)S(1)} %get-tuple-element.273), kind=kOutput, calls=%fused_computation.30.clone.1 | convolution fusion | flops 466026496 | bytes 5570564 | tf_op jit(solution)/shard_map/while/body/eval_jaxpr/ke,geo->gko/dot_general | solution.py:27
  1030.8 19.9 %fusion.52 = bf16[32,128,6656]{2,1,0:T(8,128)(2,1)} fusion(bf16[32,128,6656]{2,1,0:T(8,128)(2,1)} %get-tuple-element.265, s32[]{:T(128)S(6)} %copy.30, f32[16,6656,8]{1,2,0:T(8,128)S(1)} %fusion.51, s32[16,6656]{1,0:T(8,128)S(1)} %get-tuple-element.239, f32[6656]{0:T(1024)S(1)} %get-tuple-element.274, bf16[2,8,256]{2,1,0:T(8,128)(2,1)S(1)} %get-tuple-element.273), kind=kOutput, calls=%fused_computation.30.clone.1 | convolution fusion | flops 466026496 | bytes 5570564 | tf_op jit(solution)/shard_map/while/body/eval_jaxpr/ke,geo->gko/dot_general | solution.py:27
  1068.3 19.9 %fusion.52 = bf16[32,128,6656]{2,1,0:T(8,128)(2,1)} fusion(bf16[32,128,6656]{2,1,0:T(8,128)(2,1)} %get-tuple-element.265, s32[]{:T(128)S(6)} %copy.30, f32[16,6656,8]{1,2,0:T(8,128)S(1)} %fusion.51, s32[16,6656]{1,0:T(8,128)S(1)} %get-tuple-element.239, f32[6656]{0:T(1024)S(1)} %get-tuple-element.274, bf16[2,8,256]{2,1,0:T(8,128)(2,1)S(1)} %get-tuple-element.273), kind=kOutput, calls=%fused_computation.30.clone.1 | convolution fusion | flops 466026496 | bytes 5570564 | tf_op jit(solution)/shard_map/while/body/eval_jaxpr/ke,geo->gko/dot_general | solution.py:27
  1105.7 19.9 %fusion.52 = bf16[32,128,6656]{2,1,0:T(8,128)(2,1)} fusion(bf16[32,128,6656]{2,1,0:T(8,128)(2,1)} %get-tuple-element.265, s32[]{:T(128)S(6)} %copy.30, f32[16,6656,8]{1,2,0:T(8,128)S(1)} %fusion.51, s32[16,6656]{1,0:T(8,128)S(1)} %get-tuple-element.239, f32[6656]{0:T(1024)S(1)} %get-tuple-element.274, bf16[2,8,256]{2,1,0:T(8,128)(2,1)S(1)} %get-tuple-element.273), kind=kOutput, calls=%fused_computation.30.clone.1 | convolution fusion | flops 466026496 | bytes 5570564 | tf_op jit(solution)/shard_map/while/body/eval_jaxpr/ke,geo->gko/dot_general | solution.py:27
  1180.6 19.9 %fusion.52 = bf16[32,128,6656]{2,1,0:T(8,128)(2,1)} fusion(bf16[32,128,6656]{2,1,0:T(8,128)(2,1)} %get-tuple-element.265, s32[]{:T(128)S(6)} %copy.30, f32[16,6656,8]{1,2,0:T(8,128)S(1)} %fusion.51, s32[16,6656]{1,0:T(8,128)S(1)} %get-tuple-element.239, f32[6656]{0:T(1024)S(1)} %get-tuple-element.274, bf16[2,8,256]{2,1,0:T(8,128)(2,1)S(1)} %get-tuple-element.273), kind=kOutput, calls=%fused_computation.30.clone.1 | convolution fusion | flops 466026496 | bytes 5570564 | tf_op jit(solution)/shard_map/while/body/eval_jaxpr/ke,geo->gko/dot_general | solution.py:27
  1255.4 19.9 %fusion.52 = bf16[32,128,6656]{2,1,0:T(8,128)(2,1)} fusion(bf16[32,128,6656]{2,1,0:T(8,128)(2,1)} %get-tuple-element.265, s32[]{:T(128)S(6)} %copy.30, f32[16,6656,8]{1,2,0:T(8,128)S(1)} %fusion.51, s32[16,6656]{1,0:T(8,128)S(1)} %get-tuple-element.239, f32[6656]{0:T(1024)S(1)} %get-tuple-element.274, bf16[2,8,256]{2,1,0:T(8,128)(2,1)S(1)} %get-tuple-element.273), kind=kOutput, calls=%fused_computation.30.clone.1 | convolution fusion | flops 466026496 | bytes 5570564 | tf_op jit(solution)/shard_map/while/body/eval_jaxpr/ke,geo->gko/dot_general | solution.py:27
  1292.8 19.9 %fusion.52 = bf16[32,128,6656]{2,1,0:T(8,128)(2,1)} fusion(bf16[32,128,6656]{2,1,0:T(8,128)(2,1)} %get-tuple-element.265, s32[]{:T(128)S(6)} %copy.30, f32[16,6656,8]{1,2,0:T(8,128)S(1)} %fusion.51, s32[16,6656]{1,0:T(8,128)S(1)} %get-tuple-element.239, f32[6656]{0:T(1024)S(1)} %get-tuple-element.274, bf16[2,8,256]{2,1,0:T(8,128)(2,1)S(1)} %get-tuple-element.273), kind=kOutput, calls=%fused_computation.30.clone.1 | convolution fusion | flops 466026496 | bytes 5570564 | tf_op jit(solution)/shard_map/while/body/eval_jaxpr/ke,geo->gko/dot_general | solution.py:27
  1330.3 19.9 %fusion.52 = bf16[32,128,6656]{2,1,0:T(8,128)(2,1)} fusion(bf16[32,128,6656]{2,1,0:T(8,128)(2,1)} %get-tuple-element.265, s32[]{:T(128)S(6)} %copy.30, f32[16,6656,8]{1,2,0:T(8,128)S(1)} %fusion.51, s32[16,6656]{1,0:T(8,128)S(1)} %get-tuple-element.239, f32[6656]{0:T(1024)S(1)} %get-tuple-element.274, bf16[2,8,256]{2,1,0:T(8,128)(2,1)S(1)} %get-tuple-element.273), kind=kOutput, calls=%fused_computation.30.clone.1 | convolution fusion | flops 466026496 | bytes 5570564 | tf_op jit(solution)/shard_map/while/body/eval_jaxpr/ke,geo->gko/dot_general | solution.py:27
  1367.7 19.9 %fusion.52 = bf16[32,128,6656]{2,1,0:T(8,128)(2,1)} fusion(bf16[32,128,6656]{2,1,0:T(8,128)(2,1)} %get-tuple-element.265, s32[]{:T(128)S(6)} %copy.30, f32[16,6656,8]{1,2,0:T(8,128)S(1)} %fusion.51, s32[16,6656]{1,0:T(8,128)S(1)} %get-tuple-element.239, f32[6656]{0:T(1024)S(1)} %get-tuple-element.274, bf16[2,8,256]{2,1,0:T(8,128)(2,1)S(1)} %get-tuple-element.273), kind=kOutput, calls=%fused_computation.30.clone.1 | convolution fusion | flops 466026496 | bytes 5570564 | tf_op jit(solution)/shard_map/while/body/eval_jaxpr/ke,geo->gko/dot_general | solution.py:27
  1405.1 19.9 %fusion.52 = bf16[32,128,6656]{2,1,0:T(8,128)(2,1)} fusion(bf16[32,128,6656]{2,1,0:T(8,128)(2,1)} %get-tuple-element.265, s32[]{:T(128)S(6)} %copy.30, f32[16,6656,8]{1,2,0:T(8,128)S(1)} %fusion.51, s32[16,6656]{1,0:T(8,128)S(1)} %get-tuple-element.239, f32[6656]{0:T(1024)S(1)} %get-tuple-element.274, bf16[2,8,256]{2,1,0:T(8,128)(2,1)S(1)} %get-tuple-element.273), kind=kOutput, calls=%fused_computation.30.clone.1 | convolution fusion | flops 466026496 | bytes 5570564 | tf_op jit(solution)/shard_map/while/body/eval_jaxpr/ke,geo->gko/dot_general | solution.py:27
  1442.6 19.9 %fusion.52 = bf16[32,128,6656]{2,1,0:T(8,128)(2,1)} fusion(bf16[32,128,6656]{2,1,0:T(8,128)(2,1)} %get-tuple-element.265, s32[]{:T(128)S(6)} %copy.30, f32[16,6656,8]{1,2,0:T(8,128)S(1)} %fusion.51, s32[16,6656]{1,0:T(8,128)S(1)} %get-tuple-element.239, f32[6656]{0:T(1024)S(1)} %get-tuple-element.274, bf16[2,8,256]{2,1,0:T(8,128)(2,1)S(1)} %get-tuple-element.273), kind=kOutput, calls=%fused_computation.30.clone.1 | convolution fusion | flops 466026496 | bytes 5570564 | tf_op jit(solution)/shard_map/while/body/eval_jaxpr/ke,geo->gko/dot_general | solution.py:27
  1480.0 19.9 %fusion.52 = bf16[32,128,6656]{2,1,0:T(8,128)(2,1)} fusion(bf16[32,128,6656]{2,1,0:T(8,128)(2,1)} %get-tuple-element.265, s32[]{:T(128)S(6)} %copy.30, f32[16,6656,8]{1,2,0:T(8,128)S(1)} %fusion.51, s32[16,6656]{1,0:T(8,128)S(1)} %get-tuple-element.239, f32[6656]{0:T(1024)S(1)} %get-tuple-element.274, bf16[2,8,256]{2,1,0:T(8,128)(2,1)S(1)} %get-tuple-element.273), kind=kOutput, calls=%fused_computation.30.clone.1 | convolution fusion | flops 466026496 | bytes 5570564 | tf_op jit(solution)/shard_map/while/body/eval_jaxpr/ke,geo->gko/dot_general | solution.py:27
  1517.4 19.9 %fusion.52 = bf16[32,128,6656]{2,1,0:T(8,128)(2,1)} fusion(bf16[32,128,6656]{2,1,0:T(8,128)(2,1)} %get-tuple-element.265, s32[]{:T(128)S(6)} %copy.30, f32[16,6656,8]{1,2,0:T(8,128)S(1)} %fusion.51, s32[16,6656]{1,0:T(8,128)S(1)} %get-tuple-element.239, f32[6656]{0:T(1024)S(1)} %get-tuple-element.274, bf16[2,8,256]{2,1,0:T(8,128)(2,1)S(1)} %get-tuple-element.273), kind=kOutput, calls=%fused_computation.30.clone.1 | convolution fusion | flops 466026496 | bytes 5570564 | tf_op jit(solution)/shard_map/while/body/eval_jaxpr/ke,geo->gko/dot_general | solution.py:27
  1554.9 19.9 %fusion.52 = bf16[32,128,6656]{2,1,0:T(8,128)(2,1)} fusion(bf16[32,128,6656]{2,1,0:T(8,128)(2,1)} %get-tuple-element.265, s32[]{:T(128)S(6)} %copy.30, f32[16,6656,8]{1,2,0:T(8,128)S(1)} %fusion.51, s32[16,6656]{1,0:T(8,128)S(1)} %get-tuple-element.239, f32[6656]{0:T(1024)S(1)} %get-tuple-element.274, bf16[2,8,256]{2,1,0:T(8,128)(2,1)S(1)} %get-tuple-element.273), kind=kOutput, calls=%fused_computation.30.clone.1 | convolution fusion | flops 466026496 | bytes 5570564 | tf_op jit(solution)/shard_map/while/body/eval_jaxpr/ke,geo->gko/dot_general | solution.py:27
  1592.3 19.9 %fusion.52 = bf16[32,128,6656]{2,1,0:T(8,128)(2,1)} fusion(bf16[32,128,6656]{2,1,0:T(8,128)(2,1)} %get-tuple-element.265, s32[]{:T(128)S(6)} %copy.30, f32[16,6656,8]{1,2,0:T(8,128)S(1)} %fusion.51, s32[16,6656]{1,0:T(8,128)S(1)} %get-tuple-element.239, f32[6656]{0:T(1024)S(1)} %get-tuple-element.274, bf16[2,8,256]{2,1,0:T(8,128)(2,1)S(1)} %get-tuple-element.273), kind=kOutput, calls=%fused_computation.30.clone.1 | convolution fusion | flops 466026496 | bytes 5570564 | tf_op jit(solution)/shard_map/while/body/eval_jaxpr/ke,geo->gko/dot_general | solution.py:27
  1629.7 19.9 %fusion.52 = bf16[32,128,6656]{2,1,0:T(8,128)(2,1)} fusion(bf16[32,128,6656]{2,1,0:T(8,128)(2,1)} %get-tuple-element.265, s32[]{:T(128)S(6)} %copy.30, f32[16,6656,8]{1,2,0:T(8,128)S(1)} %fusion.51, s32[16,6656]{1,0:T(8,128)S(1)} %get-tuple-element.239, f32[6656]{0:T(1024)S(1)} %get-tuple-element.274, bf16[2,8,256]{2,1,0:T(8,128)(2,1)S(1)} %get-tuple-element.273), kind=kOutput, calls=%fused_computation.30.clone.1 | convolution fusion | flops 466026496 | bytes 5570564 | tf_op jit(solution)/shard_map/while/body/eval_jaxpr/ke,geo->gko/dot_general | solution.py:27
  1724.4 21.6 %fusion.30 = f32[128,6656]{1,0:T(8,128)} fusion(bf16[4096,6656]{1,0:T(8,128)(2,1)} %bitcast.86, bf16[128,16384]{0,1:T(8,128)(2,1)} %all-gather.5.cloned.1.call-done, s32[]{:T(128)S(6)} %select_n.7), kind=kOutput, calls=%fused_computation.39 | convolution fusion | flops 6979321856 | bytes 58982404 | tf_op jit(solution)/shard_map/dot_general | solution.py:61
  1747.0 35.5 %reduce-scatter.2.cloned.1.call-done = f32[32,6656]{1,0:T(8,128)} async-done(((f32[128,6656]{1,0:T(8,128)}), f32[32,6656]{1,0:T(8,128)}) %reduce-scatter.2.cloned.1.call-update) | async-done | bytes 851984 | tf_op jit(solution)/shard_map/reduce_scatter | solution.py:60
  (256 shorter events, 1143.2 us)
Async XLA Ops:
  7.2 443.4 %all-gather.3.cloned.1.call-start = ((), (), s32[]{:S(2)}) async-start(), calls=%async_computation.1 | async-start | bytes 1179648 | tf_op jit(solution)/shard_map/all_gather | solution.py:41
  7.9 493.6 %all-reduce.2.cloned.1.call-start = ((), (), s32[]{:S(2)}) async-start(), calls=%async_computation.2 | async-start | bytes 2097152 | tf_op jit(solution)/shard_map/psum | solution.py:44
  450.6 11.8 copy-start
  450.6 76.2 %copy-start.1 = (f32[6656]{0:T(1024)S(1)}, f32[6656]{0:T(1024)}, u32[]{:S(2)}) copy-start(f32[6656]{0:T(1024)} %param.21) | copy-start | bytes 79876
  450.6 76.2 %copy-start.2 = (bf16[2,256,8]{1,2,0:T(8,128)(2,1)S(1)}, bf16[2,256,8]{1,2,0:T(8,128)(2,1)}, u32[]{:S(2)}) copy-start(bf16[2,256,8]{1,2,0:T(8,128)(2,1)} %param.20) | copy-start | bytes 24580
  462.3 1262.2 %all-gather.5.cloned.1.call-start = ((), (), s32[]{:S(2)}) async-start(), calls=%async_computation.3 | async-start | bytes 4718592 | tf_op jit(solution)/shard_map/all_gather | solution.py:54
  526.7 1255.8 %reduce-scatter.2.cloned.1.call-start = ((), (), s32[]{:S(2)}) async-start(), calls=%async_computation.4 | async-start | bytes 4259840 | tf_op jit(solution)/shard_map/reduce_scatter | solution.py:60
Sparse Core Ops, SparseCore 0:
  10.0 42.1 all-gather.2
  462.4 39.0 all-reduce.1
  526.8 69.6 all-gather.4
  1746.1 36.3 reduce-scatter.1
where the time goes:
time: 1800 us; the launch traced here: 1790 us
  matrix products  1600 us (89%)
  waiting for transfers between devices  74.3 us (4%)
  local copies, waits for them, and re-layouts  74.2 us (4%)
  blocking collectives  21.4 us (1%)
    dot_general x128, matrix products, one_block(): jnp.einsum('ke,geo->gko', tables[book], one_hot, preferred_element_type=j...  1570 us
    dynamic_slice x64, local copies, waits for them, and re-layouts, unpack(): decoded = lax.map(one_block, code_blocks)  69.8 us
    psum x1, waiting for transfers between devices, per_device(): lax.psum(jnp.dot(features, out_weight, preferred_element_type=jnp.float32...  38.1 us
  transfers between devices with their start and end apart: 4, of which 2 were waited for; matrix products, arithmetic and copies ran while one was open for 92% of the time, Pallas kernels for 0%

commit v1 on v0

v1 whole, which is shorter than its diff:
```python
import functools
import math

import jax
import jax.numpy as jnp
from jax import lax
from jax.experimental import pallas as pl
from jax.experimental.pallas import tpu as pltpu
from jax.sharding import PartitionSpec as P

epsilon = 1e-05
LANES = 128
SUBLANES = 8
LEVELS = 16383.0
HALF = 65536.0

take_lanes = lax.GatherDimensionNumbers(
    offset_dims=(),
    collapsed_slice_dims=(1,),
    start_index_map=(1,),
    operand_batching_dims=(0,),
    start_indices_batching_dims=(0,),
)


def lookup(table, index):
    return lax.gather(
        table,
        index[..., None],
        take_lanes,
        slice_sizes=(1, 1),
        mode=lax.GatherScatterMode.PROMISE_IN_BOUNDS,
    )


def pack_books(books):
    values = books.astype(jnp.float32)
    top = jnp.maximum(jnp.max(jnp.abs(values)), 1e-30)
    levels = jnp.round(values * (LEVELS / top)).astype(jnp.int32)
    books_count, entries, group = levels.shape
    words = levels[:, :, 0::2] * 65536 + levels[:, :, 1::2]
    halves = entries // LANES
    words = words.reshape(books_count, halves, LANES, group // 2)
    words = jnp.transpose(words, (0, 1, 3, 2)).reshape(-1, LANES)
    return words, top / (LEVELS * HALF)


def decode_block(codes, tables):
    words = tables[0][0]
    picked = []
    for book, code in enumerate(codes):
        low = code < LANES
        index = code & (LANES - 1)
        first = [lookup(t, index) for t in tables[book][0]]
        second = [lookup(t, index) for t in tables[book][1]]
        picked.append([jnp.where(low, a, b) for a, b in zip(first, second)])
    rows = []
    for w in range(len(words)):
        both = picked[0][w] + picked[1][w]
        rows.append(both.astype(jnp.float32))
        rows.append((both << 16).astype(jnp.float32))
    return jnp.concatenate(rows, axis=0).astype(jnp.bfloat16)


def project_kernel(chunk, x_ref, codes_ref, table_ref, scale_ref, out_ref, x_perm, w_even, w_odd, total):
    features = x_ref.shape[1]
    width = out_ref.shape[1]
    words = table_ref.shape[0] // 4
    chunks = features // chunk
    blocks = chunk // 64

    @pl.when(pl.program_id(0) == 0)
    def _():
        row = lax.broadcasted_iota(jnp.int32, (LANES, LANES), 0)
        col = lax.broadcasted_iota(jnp.int32, (LANES, LANES), 1)
        source = (col // 64) * 64 + (col % 8) * 8 + (col % 64) // 8
        swap = jnp.where(row == source, 1.0, 0.0).astype(jnp.bfloat16)
        for c in range(features // LANES):
            at = slice(c * LANES, (c + 1) * LANES)
            x_perm[:, at] = jnp.dot(
                x_ref[:, at], swap, preferred_element_type=jnp.float32
            ).astype(jnp.bfloat16)

    def decode(c, w_ref):
        tables = [
            [
                [
                    jnp.broadcast_to(
                        table_ref[(book * 2 + half) * words + w : (book * 2 + half) * words + w + 1, :],
                        (SUBLANES, LANES),
                    )
                    for w in range(words)
                ]
                for half in range(2)
            ]
            for book in range(2)
        ]
        for b in range(blocks):
            first = pl.multiple_of(c * (chunk // 8) + b * SUBLANES, SUBLANES)
            for j in range(0, width, LANES):
                codes = [codes_ref[book, pl.ds(first, SUBLANES), j : j + LANES] for book in range(2)]
                w_ref[b * 64 : (b + 1) * 64, j : j + LANES] = decode_block(codes, tables)

    def multiply(c, w_ref):
        at = pl.ds(pl.multiple_of(c * chunk, chunk), chunk)
        total[...] += jnp.dot(x_perm[:, at], w_ref[...], preferred_element_type=jnp.float32)

    total[...] = jnp.zeros_like(total)
    w_odd[...] = jnp.zeros_like(w_odd)

    def pair(i, carry):
        decode(2 * i, w_even)
        multiply(jnp.maximum(2 * i - 1, 0), w_odd)
        decode(2 * i + 1, w_odd)
        multiply(2 * i, w_even)
        return carry

    lax.fori_loop(0, chunks // 2, pair, 0)
    multiply(chunks - 1, w_odd)
    out_ref[...] = (total[...] * scale_ref[...]).astype(out_ref.dtype)


def project(x, codes, table, scale, name, out_dtype=jnp.float32):
    rows, features = x.shape
    _, groups, outputs = codes.shape
    width = math.gcd(outputs, 512)
    chunk = min(512, features // 2)
    steps = outputs // width
    return pl.pallas_call(
        functools.partial(project_kernel, chunk),
        grid=(steps,),
        in_specs=[
            pl.BlockSpec((rows, features), lambda n: (0, 0)),
            pl.BlockSpec((2, groups, width), lambda n: (0, 0, n)),
            pl.BlockSpec(table.shape, lambda n: (0, 0)),
            pl.BlockSpec((1, width), lambda n: (0, n)),
        ],
        out_specs=pl.BlockSpec((rows, width), lambda n: (0, n)),
        out_shape=jax.ShapeDtypeStruct((rows, outputs), out_dtype),
        scratch_shapes=[
            pltpu.VMEM((rows, features), jnp.bfloat16),
            pltpu.VMEM((chunk, width), jnp.bfloat16),
            pltpu.VMEM((chunk, width), jnp.bfloat16),
            pltpu.VMEM((rows, width), jnp.float32),
        ],
        compiler_params=pltpu.CompilerParams(vmem_limit_bytes=24 * 1024 * 1024),
        cost_estimate=pl.CostEstimate(
            flops=2 * rows * features * outputs,
            bytes_accessed=8 * groups * outputs + 4 * rows * outputs + 2 * rows * features,
            transcendentals=0,
        ),
        name=name,
    )(x, codes, table, scale)


def per_device(
    attention, residual, wo_codes, wo_books, wo_scale, norm_gain, gate_codes, gate_books, gate_scale
):
    inp = lax.axis_size("inp")
    out = lax.axis_size("out")
    inp_at = lax.axis_index("inp")
    out_at = lax.axis_index("out")
    model = norm_gain.shape[0]
    features = lax.all_gather(attention, "out", axis=1, tiled=True)
    wo_table, wo_factor = pack_books(wo_books)
    gate_table, gate_factor = pack_books(gate_books)

    partial = project(features, wo_codes, wo_table, (wo_scale * wo_factor)[None, :], "wo_project")
    summed = lax.psum_scatter(partial, "inp", scatter_dimension=1, tiled=True)
    piece = summed.shape[1]
    kept = lax.dynamic_slice_in_dim(residual, inp_at * piece, piece, 1)
    hidden = kept.astype(jnp.float32) + summed
    stream = lax.all_gather(hidden.astype(jnp.bfloat16), "inp", axis=1, tiled=True)
    gain = lax.dynamic_slice_in_dim(norm_gain, (out_at * inp + inp_at) * piece, piece, 0)
    gained = (hidden * gain[None, :]).astype(jnp.bfloat16)
    squares = lax.psum(jnp.sum(hidden * hidden, axis=1, keepdims=True), ("inp", "out"))

    per_block = out // inp
    moves = [
        (q * out + o, (o // per_block) * out + (o % per_block) * inp + q)
        for q in range(inp)
        for o in range(out)
    ]
    moved = lax.ppermute(gained, ("inp", "out"), moves)
    gate_in = lax.all_gather(moved, "out", axis=1, tiled=True)
    gate_partial = project(
        gate_in, gate_codes, gate_table, (gate_scale * gate_factor)[None, :], "gate_project"
    )
    gate_sum = lax.psum_scatter(gate_partial, "inp", scatter_dimension=0, tiled=True)
    own_rows = gate_sum.shape[0]
    row_factor = lax.rsqrt(
        lax.dynamic_slice_in_dim(squares, inp_at * own_rows, own_rows, 0) / model + epsilon
    )
    gate_out = (gate_sum * row_factor).astype(jnp.bfloat16)
    return (stream, gate_out)


def solution(mesh):
    placed = (
        P(None, ("inp", "out")),
        P(None, "out"),
        P(None, "inp", "out"),
        P(),
        P("out"),
        P(),
        P(None, "inp", "out"),
        P(),
        P("out"),
    )
    return jax.shard_map(
        per_device,
        mesh=mesh,
        in_specs=placed,
        out_specs=(P(None, "out"), P("inp", "out")),
        check_vma=False,
    )
```

time: 1800 us -> 316 us (0.18)
  matrix products: 1600 us -> 0 us
  Pallas kernels: 0 us -> 123 us
  local copies, waits for them, and re-layouts: 74.2 us -> 8.18 us
  waiting for transfers between devices: 74.3 us -> 115 us
  blocking collectives: 21.4 us -> 46.5 us
    dot_general x130 -> x0, matrix products: 1600 us -> none  [the longest x128 1570 us: one_block(): jnp.einsum('ke,geo->gko', tables[book], one_hot, preferred_element_type=j...]
    pallas_call x0 -> x2, Pallas kernels: none -> 123 us  [project(): pl.pallas_call(functools.partial(project_kernel, chunk), grid=(steps,), i...]
    dynamic_slice x65 -> x1, local copies, waits for them, and re-layouts: 70.5 us -> 0.76 us  [per_device(): lax.dynamic_slice_in_dim(norm_gain, (out_at * inp + inp_at) * piece, piec...]
    all_gather x1, waiting for transfers between devices: 0.01 us -> 50.7 us  [per_device(): gate_in = lax.all_gather(moved, 'out', axis=1, tiled=True)]
    all_gather x1, waiting for transfers between devices: 0.02 us -> 40.8 us  [per_device(): features = lax.all_gather(attention, 'out', axis=1, tiled=True)]
    psum x1 -> x0, waiting for transfers between devices: 38.1 us -> none  [per_device(): lax.psum(jnp.dot(features, out_weight, preferred_element_type=jnp.float32...]
  transfers between devices with their start and end apart: 4 -> 5, of which waited for: 2 -> 3; matrix products, arithmetic and copies ran while one was open for 92% -> 1% of each run, Pallas kernels for 0% -> 0%
where the time goes in v1:
time: 316 us
  Pallas kernels  123 us (39%)
  waiting for transfers between devices  115 us (36%)
  blocking collectives  46.5 us (15%)
  between operations  15.2 us (5%)
  local copies, waits for them, and re-layouts  8.18 us (3%)
  other arithmetic  6.56 us (2%)
    pallas_call x2, Pallas kernels, project(): pl.pallas_call(functools.partial(project_kernel, chunk), grid=(steps,), i...  123 us
    all_gather x1, waiting for transfers between devices, per_device(): gate_in = lax.all_gather(moved, 'out', axis=1, tiled=True)  50.7 us
    all_gather x1, waiting for transfers between devices, per_device(): features = lax.all_gather(attention, 'out', axis=1, tiled=True)  40.8 us
    psum x1, blocking collectives, per_device(): lax.psum(jnp.sum(hidden * hidden, axis=1, keepdims=True), ('inp', 'out'))  39.2 us
    reduce_scatter x1, waiting for transfers between devices, per_device(): summed = lax.psum_scatter(partial, 'inp', scatter_dimension=1, tiled=True)  23.1 us
    unnamed x13, local copies, waits for them, and re-layouts  7.32 us
    all_gather x1, blocking collectives, per_device(): lax.all_gather(hidden.astype(jnp.bfloat16), 'inp', axis=1, tiled=True)  7.28 us
  transfers between devices with their start and end apart: 5, of which 3 were waited for; matrix products, arithmetic and copies ran while one was open for 1% of the time, Pallas kernels for 0%

profile of v1, /device:TPU:0, one launch (start us, length us, event | category | flops | bytes accessed | tf_op | source)
XLA Modules:
  0.0 315.7 jit_solution(12918625420759351193)
XLA Ops:
  7.2 0.0 all-gather.3.cloned.1.call-start
  7.2 0.7 all-gather.3.cloned.1.call-update
  7.9 0.0 reduce-scatter.3.cloned.1.call-start
  8.0 1.3 fusion.1
  10.0 0.7 fusion.3
  10.7 0.7 broadcast_multiply_fusion.1
  11.4 40.8 %all-gather.3.cloned.1.call-done.x_ref = bf16[128,4096]{1,0:T(8,128)(2,1)} async-done(((bf16[128,512]{1,0:T(8,128)(2,1)}), bf16[128,4096]{1,0:T(8,128)(2,1)}) %all-gather.3.cloned.1.call-update) | async-done | bytes 1048592 | tf_op jit(solution)/shard_map/all_gather | solution.py:164
  52.2 3.4 %copy-done = s32[2,512,2048]{2,1,0:T(8,128)S(1)} copy-done((s32[2,512,2048]{2,1,0:T(8,128)S(1)}, s32[2,512,2048]{2,1,0:T(8,128)}, u32[]{:S(2)}) %copy-start) | copy-done | bytes 8388632
  55.6 1.2 copy-done.2
  56.8 29.6 %wo_project.1 = f32[128,2048]{1,0:T(8,128)} custom-call(bf16[128,4096]{1,0:T(8,128)(2,1)S(1)} %copy-done.2, s32[2,512,2048]{2,1,0:T(8,128)S(1)} %copy-done, s32[16,128]{1,0:T(8,128)S(1)} %bitcast.15, f32[1,2048]{1,0:T(1,128)S(1)} %bitcast.16), custom_call_target="tpu_custom_call" | custom-call | flops 2147483648 | bytes 10485760 | tf_op jit(solution)/shard_map/wo_project/pallas_call | solution.py:129
  86.4 0.0 reduce-scatter.3.cloned.1.call-update
  86.4 0.0 all-gather.5.cloned.1.call-start
  86.5 0.8 dynamic_slice.10
  87.2 23.1 %reduce-scatter.3.cloned.1.call-done = f32[128,512]{1,0:T(8,128)} async-done(((f32[128,2048]{1,0:T(8,128)}), f32[128,512]{1,0:T(8,128)}) %reduce-scatter.3.cloned.1.call-update) | async-done | bytes 262160 | tf_op jit(solution)/shard_map/reduce_scatter | solution.py:169
  110.4 1.1 multiply_reduce_fusion
  111.5 0.7 collective-permute-start
  112.2 0.0 collective-permute-done
  112.2 0.0 copy-start.3
  112.2 0.6 copy-done.3
  112.8 0.0 all-gather.5.cloned.1.call-update
  112.9 0.0 reduce-scatter.5.cloned.1.call-start
  112.9 0.0 copy-done.4
  112.9 0.6 fusion.4
  114.3 50.7 %all-gather.5.cloned.1.call-done.x_ref = bf16[128,4096]{1,0:T(8,128)(2,1)} async-done(((bf16[128,512]{1,0:T(8,128)(2,1)}), bf16[128,4096]{1,0:T(8,128)(2,1)}) %all-gather.5.cloned.1.call-update) | async-done | bytes 1048592 | tf_op jit(solution)/shard_map/all_gather | solution.py:185
  165.0 1.2 copy-done.1
  166.2 93.5 %gate_project.1 = f32[128,6656]{1,0:T(8,128)} custom-call(bf16[128,4096]{1,0:T(8,128)(2,1)S(1)} %copy-done.1, s32[2,512,6656]{2,1,0:T(8,128)} %codes_ref.3, s32[16,128]{1,0:T(8,128)S(1)} %bitcast.14, f32[1,6656]{1,0:T(1,128)S(1)} %broadcast_in_dim.11.scale_ref), custom_call_target="tpu_custom_call" | custom-call | flops 6979321856 | bytes 31719424 | tf_op jit(solution)/shard_map/gate_project/pallas_call | solution.py:129
  259.7 0.0 reduce-scatter.5.cloned.1.call-update
  259.8 7.3 %all_gather.10 = bf16[128,2048]{1,0:T(8,128)(2,1)S(1)} all-gather(bf16[128,512]{1,0:T(8,128)(2,1)S(1)} %get-tuple-element.4), channel_id=1, replica_groups=mesh['inp'=4,'out'=8] {'inp'}, dimensions={1}, use_global_device_ids=true | all-gather | bytes 655360 | tf_op jit(solution)/shard_map/all_gather | solution.py:173
  267.1 39.2 %psum.7 = f32[128,1]{0,1:T(1,128)S(1)} all-reduce(f32[128,1]{0,1:T(1,128)S(1)} %bitcast.17), channel_id=1, replica_groups=mesh['inp'=4,'out'=8] {'inp','out'}, use_global_device_ids=true, to_apply=%region_5.6 | all-reduce | flops 128 | bytes 1024 | tf_op jit(solution)/shard_map/psum | solution.py:176
  306.3 0.1 rsqrt_bitcast_fusion
  306.4 2.0 multiply_convert_fusion
  308.4 0.8 copy.14
  (16 shorter events, 0.1 us)
Async XLA Ops:
  7.2 105.7 %copy-start.4 = (bf16[2,256,8]{1,2,0:T(8,128)(2,1)S(1)}, bf16[2,256,8]{1,2,0:T(8,128)(2,1)}, u32[]{:S(2)}) copy-start(bf16[2,256,8]{1,2,0:T(8,128)(2,1)} %param.16) | copy-start | bytes 24580
  7.2 107.1 %copy-start.5 = (f32[6656]{0:T(1024)S(1)}, f32[6656]{0:T(1024)}, u32[]{:S(2)}) copy-start(f32[6656]{0:T(1024)} %param.17) | copy-start | bytes 79876
  7.2 45.0 %all-gather.3.cloned.1.call-start = ((), (), s32[]{:S(2)}) async-start(), calls=%async_computation.2 | async-start | bytes 1179648 | tf_op jit(solution)/shard_map/all_gather | solution.py:164
  7.9 102.5 %reduce-scatter.3.cloned.1.call-start = ((), (), s32[]{:S(2)}) async-start(), calls=%async_computation.3 | async-start | bytes 1310720 | tf_op jit(solution)/shard_map/reduce_scatter | solution.py:169
  52.2 3.4 %copy-start = (s32[2,512,2048]{2,1,0:T(8,128)S(1)}, s32[2,512,2048]{2,1,0:T(8,128)}, u32[]{:S(2)}) copy-start(s32[2,512,2048]{2,1,0:T(8,128)} %codes_ref.2) | copy-start | bytes 25165828
  55.6 1.2 copy-start.2
  86.4 78.6 %all-gather.5.cloned.1.call-start = ((), (), s32[]{:S(2)}) async-start(), calls=%async_computation.4 | async-start | bytes 1179648 | tf_op jit(solution)/shard_map/all_gather | solution.py:185
  111.5 0.7 collective-permute-start
  112.2 0.7 copy-start.3
  112.9 193.5 %reduce-scatter.5.cloned.1.call-start = ((), (), s32[]{:S(2)}) async-start(), calls=%async_computation.5 | async-start | bytes 4259840 | tf_op jit(solution)/shard_map/reduce_scatter | solution.py:189
  165.0 1.2 copy-start.1
Sparse Core Ops, SparseCore 0:
  10.0 42.1 all-gather.2
  86.5 23.7 reduce-scatter.2
  113.0 51.9 all-gather.4
  259.9 38.8 reduce-scatter.4
